TPU v7x, 256 devices: a whole 4x4x8 slice. The times are simulated.
256 devices in a mesh: section: 4 (over y), seq: 64 (over z, x, core).
Axes of the slice: x: 4, y: 4, z: 8, core: 2. Of those that a mesh axis runs over, the one named last changes fastest.
Arguments:
- patches: bfloat16 [64, 729, 1152], P('seq'), may hold values from -40 to 40
- fc_gain: float32 [4, 1152], P('section'), may hold values from 0.1 to 1.9
- fc_in: bfloat16 [4, 1152, 2176], P('section', 'seq'), may hold values from -0.1875 to 0.1875
- fc_in_bias: float32 [4, 2176], P('section'), may hold values from -3 to 3
- fc_out: bfloat16 [4, 2176, 1152], P('section', None, 'seq'), may hold values from -0.125 to 0.125
- fc_out_bias: float32 [4, 1152], P('section'), may hold values from -3 to 3
- proj_weight: bfloat16 [1152, 3584], P('seq'), may hold values from -0.1875 to 0.1875
- text_embed: bfloat16 [8192, 3584], P('seq'), may hold values from -40 to 40
- frame_start: int32 [64], replicated, may hold values from 0 to 8191, as said below
- frame_count: int32 [64], replicated, may hold values from 1 to 196, as said below
- segment_ids: int32 [8192], replicated, may hold values from 0 to 2, as said below
- norm_gain: float32 [3584], replicated, may hold values from 0.1 to 1.9
- query_weight: bfloat16 [3584, 2048], P(None, 'section'), may hold values from -3 to 3
- query_bias: float32 [2048], P('section'), may hold values from -3 to 3
- key_weight: bfloat16 [3584, 512], P(None, 'section'), may hold values from -1 to 1
- value_weight: bfloat16 [3584, 512], P(None, 'section'), may hold values from -0.09375 to 0.09375
- value_bias: float32 [512], P('section'), may hold values from -3 to 3
Outputs:
- attended: bfloat16 [8192, 2048], P('seq', 'section')
Inputs may be any that keep to these rules, and one draw needn't show every extreme that they name: Frame f keeps its first frame_count[f] pooled tokens and places them at positions frame_start[f] to frame_start[f] + frame_count[f] - 1; frame f begins in shard f, at a position from f * 128 to (f + 1) * 128 - 1; every frame ends before the next one begins, and the last ends by position 8191. The frame of shard 64 / 2 - 1 runs into the next shard. `frame_count`: some frame keeps all 196 tokens. `segment_ids`: segment numbers never fall along the sequence, and each of 0, 1 and 2 occurs.
All inputs are finite; a program needn't handle non-finite values.
Results may differ from a plain program's by a relative error of at most 0.02.
Values may be sent and summed in bfloat16 or wider, within the bound.
No kernel may reach another device: no remote copies, remote signals or barrier semaphores. Data moves between devices by JAX's collectives and lax.ppermute only.
A program may use at most 128 MiB of HBM per device.

v0:
```python
import math
import jax
import jax.numpy as jnp
from jax import lax
from jax.sharding import PartitionSpec as P

GRID = 27
layer_eps = 1e-06
rms_eps = 1e-06
rope_base = 1000000.0
mask_floor = -1e30


def turned_gather(arrays, axis, dims):
    turned = [jnp.moveaxis(a, dim, 0) for a, dim in zip(arrays, dims)]
    both = jnp.concatenate([t.reshape(len(t), -1) for t in turned], axis=1)
    filled, at, finished = (lax.all_gather(both, axis, axis=0, tiled=True), 0, [])
    for t, dim in zip(turned, dims):
        section = filled[:, at : at + t[0].size].reshape(-1, *t.shape[1:])
        finished.append(jnp.moveaxis(section, 0, dim))
        at += t[0].size
    return tuple(finished)


def passed_along(block, axis, distance):
    devices = range(lax.axis_size(axis))
    route = [(i - distance, i) for i in devices if i - distance in devices]
    return lax.ppermute(block, axis, route)


def from_root(x, axis, root):
    return lax.dynamic_index_in_dim(lax.all_gather(x, axis), root, 0, keepdims=False)


def layer_norm(values, scales):
    widened = values.astype(jnp.float32)
    center = widened - jnp.mean(widened, axis=-1, keepdims=True)
    spread = jnp.mean(center * center, axis=-1, keepdims=True)
    return center * lax.rsqrt(spread + layer_eps) * scales


def encoder_layer(values, scales, w_in, b_in, w_out, b_out):
    normed = layer_norm(values, scales).astype(jnp.bfloat16)
    hidden = jax.nn.gelu(
        jnp.dot(normed, w_in, preferred_element_type=jnp.float32) + b_in, approximate=True
    ).astype(jnp.bfloat16)
    summed = (
        values.astype(jnp.float32)
        + jnp.dot(hidden, w_out, preferred_element_type=jnp.float32)
        + b_out
    )
    return summed.astype(jnp.bfloat16)


def pool_frame(encoded):
    channel = encoded.shape[-1]
    grid_side = GRID
    pool_side = (GRID + 1) // 2
    grid_cells = encoded.astype(jnp.float32).reshape(grid_side, grid_side, channel)
    pad_cells = 2 * pool_side - grid_side
    grid_cells = jnp.pad(grid_cells, [(0, pad_cells), (0, pad_cells), (0, 0)])
    totals = grid_cells.reshape(pool_side, 2, pool_side, 2, channel).sum(axis=(1, 3))
    counts = jnp.minimum(2, grid_side - 2 * jnp.arange(pool_side)).astype(jnp.float32)
    cell_area = counts[:, None] * counts[None, :]
    return (totals / cell_area[..., None]).reshape(pool_side * pool_side, channel)


def rotate(values, positions):
    head_dim = values.shape[-1]
    half_dim = head_dim // 2
    inv_rates = jnp.exp(
        jnp.arange(half_dim, dtype=jnp.float32) * (-2.0 * math.log(rope_base) / head_dim)
    )
    angles = positions.astype(jnp.float32)[:, None] * inv_rates[None, :]
    cosine = jnp.cos(angles)[:, None, :]
    sine_part = jnp.sin(angles)[:, None, :]
    first_half = values[..., :half_dim]
    second = values[..., half_dim:]
    return jnp.concatenate(
        [first_half * cosine - second * sine_part, second * cosine + first_half * sine_part],
        axis=-1,
    )


def take_rows(source, offsets, upper_limit):
    is_valid = (offsets >= 0) & (offsets < upper_limit)
    picked = jnp.take(source, jnp.clip(offsets, 0, source.shape[0] - 1), axis=0)
    return (jnp.where(is_valid[:, None], picked, jnp.zeros((), source.dtype)), is_valid)


def attend_block(softmax_state, queries, query_pos, query_seg, key_block, block_start, segment_ids):
    row_top, row_total, row_acc = softmax_state
    head_dim = queries.shape[1]
    key_part = key_block[:, :head_dim]
    value_part = key_block[:, head_dim:]
    scores = lax.dot_general(
        queries, key_part, (((1,), (1,)), ((), ())), preferred_element_type=jnp.float32
    )
    scores = scores * (1.0 / math.sqrt(head_dim))
    key_pos = block_start + jnp.arange(key_block.shape[0], dtype=jnp.int32)
    key_seg = lax.dynamic_slice_in_dim(segment_ids, block_start, key_block.shape[0], 0)
    allowed = (key_pos[None, :] <= query_pos[:, None]) & (key_seg[None, :] == query_seg[:, None])
    masked = jnp.where(allowed, scores, mask_floor)
    new_top = jnp.maximum(row_top, jnp.max(masked, axis=1))
    weights = jnp.where(allowed, jnp.exp(masked - new_top[:, None]), 0.0)
    keep_old = jnp.exp(row_top - new_top)
    row_total = row_total * keep_old + jnp.sum(weights, axis=1)
    row_acc = row_acc * keep_old[:, None] + jnp.dot(
        weights.astype(jnp.bfloat16), value_part, preferred_element_type=jnp.float32
    )
    return (new_top, row_total, row_acc)


def per_device(
    patches,
    fc_gain,
    fc_in,
    fc_in_bias,
    fc_out,
    fc_out_bias,
    proj_weight,
    text_embed,
    frame_start,
    frame_count,
    segment_ids,
    norm_gain,
    query_weight,
    query_bias,
    key_weight,
    value_weight,
    value_bias,
):
    section_count = lax.axis_size("section")
    section_id = lax.axis_index("section")
    shard_count = lax.axis_size("seq")
    shard_id = lax.axis_index("seq")
    shard_rows = text_embed.shape[0]
    model_width = text_embed.shape[1]
    head_size = key_weight.shape[1]
    group_size = query_weight.shape[1] // head_size
    frame_patches = patches[0]
    patch_rows, feature_width = frame_patches.shape
    column_count = model_width // section_count
    proj_block = lax.dynamic_slice_in_dim(proj_weight, section_id * column_count, column_count, 1)
    w_in, w_out, proj_full = turned_gather((fc_in, fc_out, proj_block), "seq", (1, 2, 0))
    w_in = w_in[0]
    w_out = w_out[0]
    layer_gain = fc_gain[0]
    bias_in = fc_in_bias[0]
    bias_out = fc_out_bias[0]
    band_rows = 9
    batch_rows = band_rows * GRID
    batches = GRID // band_rows
    tick_count = batches + section_count - 1
    first_section = section_id == 0
    last_section = section_id == section_count - 1

    def run_tick(tick_index, loop_carry):
        inflow, collected = loop_carry
        feed_rows = lax.dynamic_slice_in_dim(
            frame_patches, jnp.minimum(tick_index, batches - 1) * batch_rows, batch_rows, 0
        )
        result = encoder_layer(
            jnp.where(first_section, feed_rows, inflow), layer_gain, w_in, bias_in, w_out, bias_out
        )
        slot_start = jnp.clip(tick_index - section_count + 1, 0, batches - 1) * batch_rows
        current = lax.dynamic_slice_in_dim(collected, slot_start, batch_rows, 0)
        is_ready = last_section & (tick_index >= section_count - 1)
        collected = lax.dynamic_update_slice_in_dim(
            collected, jnp.where(is_ready, result, current), slot_start, 0
        )
        inflow = passed_along(result, "section", 1)
        return (inflow, collected)

    start_state = (
        jnp.zeros((batch_rows, feature_width), jnp.bfloat16),
        jnp.zeros((patch_rows, feature_width), jnp.bfloat16),
    )
    inflow, collected = lax.fori_loop(0, tick_count, run_tick, start_state)
    pooled = pool_frame(collected).astype(jnp.bfloat16)
    local_slots = jnp.arange(shard_rows, dtype=jnp.int32)
    positions = shard_id * shard_rows + local_slots
    own_start = frame_start[shard_id]
    own_count = frame_count[shard_id]
    previous = jnp.maximum(shard_id - 1, 0)
    prev_offsets = positions - frame_start[previous]
    prev_valid = (shard_id > 0) & (prev_offsets >= 0) & (prev_offsets < frame_count[previous])
    own_rows, own_valid = take_rows(pooled, positions - own_start, own_count)
    sent_rows, sent_valid = take_rows(pooled, positions + shard_rows - own_start, own_count)
    arrived = passed_along(sent_rows, "seq", 1)
    vision = jnp.where(own_valid[:, None], own_rows, arrived)
    vision = from_root(vision, "section", section_count - 1)
    block_cols = jnp.dot(vision, proj_full, preferred_element_type=jnp.float32).astype(jnp.bfloat16)
    text_cols = lax.dynamic_slice_in_dim(text_embed, section_id * column_count, column_count, 1)
    mixed_cols = jnp.where((own_valid | prev_valid)[:, None], block_cols, text_cols)
    inputs = lax.all_gather(mixed_cols, "section", axis=1, tiled=True)
    widened = inputs.astype(jnp.float32)
    normed = (
        widened
        * lax.rsqrt(jnp.mean(widened * widened, axis=1, keepdims=True) + rms_eps)
        * norm_gain
    ).astype(jnp.bfloat16)
    queries = jnp.dot(normed, query_weight, preferred_element_type=jnp.float32) + query_bias
    queries = rotate(queries.reshape(shard_rows, group_size, head_size), positions).astype(
        jnp.bfloat16
    )
    queries = queries.reshape(shard_rows * group_size, head_size)
    key_heads = jnp.dot(normed, key_weight, preferred_element_type=jnp.float32)
    key_heads = rotate(key_heads.reshape(shard_rows, 1, head_size), positions).astype(jnp.bfloat16)
    key_heads = key_heads.reshape(shard_rows, head_size)
    values = (
        jnp.dot(normed, value_weight, preferred_element_type=jnp.float32) + value_bias
    ).astype(jnp.bfloat16)
    stacked = jnp.concatenate([key_heads, values], axis=1)
    query_pos = jnp.repeat(positions, group_size)
    query_seg = jnp.repeat(
        lax.dynamic_slice_in_dim(segment_ids, shard_id * shard_rows, shard_rows, 0), group_size
    )
    query_total = shard_rows * group_size
    blank_state = (
        jnp.full((query_total,), mask_floor, jnp.float32),
        jnp.zeros((query_total,), jnp.float32),
        jnp.zeros((query_total, head_size), jnp.float32),
    )
    half_count = shard_count // 2
    is_lower = shard_id < half_count
    quarter = shard_count // 4
    partner_queries = passed_along(queries, "seq", -half_count)
    partner_id = shard_id + half_count
    partner_pos = jnp.repeat(partner_id * shard_rows + local_slots, group_size)
    partner_seg = jnp.repeat(
        lax.dynamic_slice_in_dim(
            segment_ids, jnp.minimum(partner_id, shard_count - 1) * shard_rows, shard_rows, 0
        ),
        group_size,
    )
    own_low = jnp.where(is_lower, 0, quarter * shard_rows)
    own_high = (shard_id + 1) * shard_rows
    part_high = jnp.where(is_lower, quarter * shard_rows, 0)

    def visit_pair(pair_state, key_block, block_start):
        own_state, other_state = pair_state
        own_state = lax.cond(
            (block_start >= own_low) & (block_start < own_high),
            lambda carried: attend_block(
                carried, queries, query_pos, query_seg, key_block, block_start, segment_ids
            ),
            lambda carried: carried,
            own_state,
        )
        other_state = lax.cond(
            block_start < part_high,
            lambda carried: attend_block(
                carried,
                partner_queries,
                partner_pos,
                partner_seg,
                key_block,
                block_start,
                segment_ids,
            ),
            lambda carried: carried,
            other_state,
        )
        return (own_state, other_state)

    initial = (blank_state, blank_state)
    arrived_rows = lax.all_gather(stacked, "seq", axis=0, tiled=True)
    sub_rows = math.gcd(arrived_rows.shape[0], shard_rows)

    def visit_one(block_index, inner_state):
        key_block = lax.dynamic_slice_in_dim(arrived_rows, block_index * sub_rows, sub_rows, 0)
        return visit_pair(inner_state, key_block, block_index * sub_rows)

    folded = lax.fori_loop(0, arrived_rows.shape[0] // sub_rows, visit_one, initial)
    own_state, other_state = folded
    back_top, back_total, back_acc = passed_along(
        (other_state[0], other_state[1], other_state[2]), "seq", half_count
    )
    back_top = jnp.where(is_lower, mask_floor, back_top)
    back_total = jnp.where(is_lower, 0.0, back_total)
    back_acc = jnp.where(is_lower, 0.0, back_acc)
    own_top, own_total, own_acc = own_state
    row_top = jnp.maximum(own_top, back_top)
    keep_own = jnp.exp(own_top - row_top)
    keep_back = jnp.exp(back_top - row_top)
    row_total = own_total * keep_own + back_total * keep_back
    row_acc = own_acc * keep_own[:, None] + back_acc * keep_back[:, None]
    attended = (row_acc / row_total[:, None]).astype(jnp.bfloat16)
    return attended.reshape(shard_rows, group_size * head_size)


def solution(mesh):
    return jax.shard_map(
        per_device,
        mesh=mesh,
        in_specs=(
            P("seq", None, None),
            P("section", None),
            P("section", "seq", None),
            P("section", None),
            P("section", None, "seq"),
            P("section", None),
            P("seq", None),
            P("seq", None),
            P(),
            P(),
            P(),
            P(),
            P(None, "section"),
            P("section"),
            P(None, "section"),
            P(None, "section"),
            P("section"),
        ),
        out_specs=P("seq", "section"),
        check_vma=False,
    )
```

profile of v0, /device:TPU:231, one launch (start us, length us, event | category | flops | bytes accessed | tf_op | source)
XLA Modules:
  0.0 614.5 jit_solution(5960631140011287223)
XLA Ops:
  13.4 91.2 %all-gather.10.cloned.1.call-done = bf16[64,18,5248]{2,1,0:T(8,128)(2,1)} async-done(((bf16[1,18,5248]{2,1,0:T(8,128)(2,1)}), bf16[64,18,5248]{2,1,0:T(8,128)(2,1)}) %all-gather.10.cloned.1.call-update) | async-done | bytes 12091408 | tf_op jit(solution)/shard_map/all_gather | solution.py:17
  104.6 17.1 %reshape.296 = bf16[1152,5248]{1,0:T(8,128)(2,1)} reshape(bf16[64,18,5248]{2,1,0:T(8,128)(2,1)} %all-gather.10.cloned.1.call-done) | data formatting | bytes 24182784
  121.7 8.4 %slice_bitcast_fusion = (bf16[2176,1152]{0,1:T(8,128)(2,1)}, bf16[1152,2176]{1,0:T(8,128)(2,1)}) fusion(bf16[1152,5248]{1,0:T(8,128)(2,1)} %reshape.296), kind=kLoop, calls=%fused_computation.76 | loop fusion | bytes 20054016 | tf_op jit(solution)/shard_map/squeeze | solution.py:147
  130.1 8.5 %copy.23 = bf16[2176,1152]{1,0:T(8,128)(2,1)} copy(bf16[2176,1152]{0,1:T(8,128)(2,1)} %get-tuple-element.956) | data formatting | bytes 10027008 | tf_op jit(solution)/shard_map/while | solution.py:179
  140.0 138.9 %while.43 = (s32[]{:T(128)}, bf16[243,1152]{1,0:T(8,128)(2,1)S(1)}, bf16[729,1152]{1,0:T(8,128)(2,1)}, pred[]{:T(512)}, bf16[729,1152]{1,0:T(8,128)(2,1)}, /*ind...) while((s32[]{:T(128)}, bf16[243,1152]{1,0:T(8,128)(2,1)S(1)}, ...), condition=%wide.region_3.4_spmd, body=%wide.region_0.3_spmd.sunk | while | flops 2446610432 | bytes 18521884 | solution.py:179
  141.8 7.5 %dynamic-slice_select_fusion.4 = (bf16[243,1152]{1,0:T(8,128)(2,1)S(1)}, bf16[243,1152]{1,0:T(8,128)(2,1)S(1)}) fusion(bf16[729,1152]{1,0:T(8,128)(2,1)} %get-tuple-element.1202, s32[]{:T(128)S(6)} %select_n.249, pred[]{:T(512)S(6)} %and.105, f32[1152]{0:T(1024)S(1)} %reduce.8, bf16[2176,1152]{1,0:T(8,128)(2,1)} %get-tuple-element.1227, ...), kind=kOutput, calls=%fused_computation.65.clone.1 | convolution fusion | flops 2444650496 | bytes 12880133 | tf_op jit(solution)/shard_map/while/body/eval_jaxpr/dot_general | solution.py:49
  152.5 3.4 dynamic_update_slice.14
  156.0 8.5 %collective-permute-done = bf16[243,1152]{1,0:T(8,128)(2,1)S(1)} collective-permute-done((bf16[243,1152]{1,0:T(8,128)(2,1)S(1)}, bf16[243,1152]{1,0:T(8,128)(2,1)S(1)}, u32[]{:S(2)}, u32[]{:S(2)}) %collective-permute-start) | collective-permute-done | bytes 559904 | tf_op jit(solution)/shard_map/while/body/eval_jaxpr/ppermute | solution.py:28
  166.3 7.5 %dynamic-slice_select_fusion.4 = (bf16[243,1152]{1,0:T(8,128)(2,1)S(1)}, bf16[243,1152]{1,0:T(8,128)(2,1)S(1)}) fusion(bf16[729,1152]{1,0:T(8,128)(2,1)} %get-tuple-element.1202, s32[]{:T(128)S(6)} %select_n.249, pred[]{:T(512)S(6)} %and.105, f32[1152]{0:T(1024)S(1)} %reduce.8, bf16[2176,1152]{1,0:T(8,128)(2,1)} %get-tuple-element.1227, ...), kind=kOutput, calls=%fused_computation.65.clone.1 | convolution fusion | flops 2444650496 | bytes 12880133 | tf_op jit(solution)/shard_map/while/body/eval_jaxpr/dot_general | solution.py:49
  173.8 4.1 collective-permute-start
  178.0 3.4 dynamic_update_slice.14
  181.4 7.7 %collective-permute-done = bf16[243,1152]{1,0:T(8,128)(2,1)S(1)} collective-permute-done((bf16[243,1152]{1,0:T(8,128)(2,1)S(1)}, bf16[243,1152]{1,0:T(8,128)(2,1)S(1)}, u32[]{:S(2)}, u32[]{:S(2)}) %collective-permute-start) | collective-permute-done | bytes 559904 | tf_op jit(solution)/shard_map/while/body/eval_jaxpr/ppermute | solution.py:28
  190.9 7.5 %dynamic-slice_select_fusion.4 = (bf16[243,1152]{1,0:T(8,128)(2,1)S(1)}, bf16[243,1152]{1,0:T(8,128)(2,1)S(1)}) fusion(bf16[729,1152]{1,0:T(8,128)(2,1)} %get-tuple-element.1202, s32[]{:T(128)S(6)} %select_n.249, pred[]{:T(512)S(6)} %and.105, f32[1152]{0:T(1024)S(1)} %reduce.8, bf16[2176,1152]{1,0:T(8,128)(2,1)} %get-tuple-element.1227, ...), kind=kOutput, calls=%fused_computation.65.clone.1 | convolution fusion | flops 2444650496 | bytes 12880133 | tf_op jit(solution)/shard_map/while/body/eval_jaxpr/dot_general | solution.py:49
  198.4 4.1 collective-permute-start
  206.0 6.8 %collective-permute-done = bf16[243,1152]{1,0:T(8,128)(2,1)S(1)} collective-permute-done((bf16[243,1152]{1,0:T(8,128)(2,1)S(1)}, bf16[243,1152]{1,0:T(8,128)(2,1)S(1)}, u32[]{:S(2)}, u32[]{:S(2)}) %collective-permute-start) | collective-permute-done | bytes 559904 | tf_op jit(solution)/shard_map/while/body/eval_jaxpr/ppermute | solution.py:28
  214.6 7.5 %dynamic-slice_select_fusion.4 = (bf16[243,1152]{1,0:T(8,128)(2,1)S(1)}, bf16[243,1152]{1,0:T(8,128)(2,1)S(1)}) fusion(bf16[729,1152]{1,0:T(8,128)(2,1)} %get-tuple-element.1202, s32[]{:T(128)S(6)} %select_n.249, pred[]{:T(512)S(6)} %and.105, f32[1152]{0:T(1024)S(1)} %reduce.8, bf16[2176,1152]{1,0:T(8,128)(2,1)} %get-tuple-element.1227, ...), kind=kOutput, calls=%fused_computation.65.clone.1 | convolution fusion | flops 2444650496 | bytes 12880133 | tf_op jit(solution)/shard_map/while/body/eval_jaxpr/dot_general | solution.py:49
  222.2 4.1 collective-permute-start
  229.8 6.0 collective-permute-done
  237.5 7.5 %dynamic-slice_select_fusion.4 = (bf16[243,1152]{1,0:T(8,128)(2,1)S(1)}, bf16[243,1152]{1,0:T(8,128)(2,1)S(1)}) fusion(bf16[729,1152]{1,0:T(8,128)(2,1)} %get-tuple-element.1202, s32[]{:T(128)S(6)} %select_n.249, pred[]{:T(512)S(6)} %and.105, f32[1152]{0:T(1024)S(1)} %reduce.8, bf16[2176,1152]{1,0:T(8,128)(2,1)} %get-tuple-element.1227, ...), kind=kOutput, calls=%fused_computation.65.clone.1 | convolution fusion | flops 2444650496 | bytes 12880133 | tf_op jit(solution)/shard_map/while/body/eval_jaxpr/dot_general | solution.py:49
  245.1 4.1 collective-permute-start
  252.7 5.1 collective-permute-done
  259.6 7.5 %dynamic-slice_select_fusion.4 = (bf16[243,1152]{1,0:T(8,128)(2,1)S(1)}, bf16[243,1152]{1,0:T(8,128)(2,1)S(1)}) fusion(bf16[729,1152]{1,0:T(8,128)(2,1)} %get-tuple-element.1202, s32[]{:T(128)S(6)} %select_n.249, pred[]{:T(512)S(6)} %and.105, f32[1152]{0:T(1024)S(1)} %reduce.8, bf16[2176,1152]{1,0:T(8,128)(2,1)} %get-tuple-element.1227, ...), kind=kOutput, calls=%fused_computation.65.clone.1 | convolution fusion | flops 2444650496 | bytes 12880133 | tf_op jit(solution)/shard_map/while/body/eval_jaxpr/dot_general | solution.py:49
  267.1 4.1 collective-permute-start
  274.7 4.2 collective-permute-done
  283.8 5.5 reshape.273
  289.3 4.5 reduce_sum.76
  304.7 33.4 %all-gather.8.cloned.1.call-done = bf16[512,1152]{1,0:T(8,128)(2,1)} async-done(((bf16[128,1152]{1,0:T(8,128)(2,1)}), bf16[512,1152]{1,0:T(8,128)(2,1)}) %all-gather.8.cloned.1.call-update) | async-done | bytes 1179664 | tf_op jit(solution)/shard_map/all_gather | solution.py:32
  340.3 12.5 %all_gather.18 = bf16[128,3584]{1,0:T(8,128)(2,1)S(1)} all-gather(bf16[128,896]{1,0:T(8,128)(2,1)S(1)} %fusion.69), channel_id=1, replica_groups=mesh['section'=4,'seq'=64] {'section'}, dimensions={1}, use_global_device_ids=true | all-gather | bytes 1146880 | tf_op jit(solution)/shard_map/all_gather | solution.py:196
  358.7 4.5 collective-permute-start.2
  365.2 70.4 %all-gather.6.cloned.1.call-done = bf16[8192,256]{0,1:T(8,128)(2,1)} async-done(((bf16[128,256]{0,1:T(8,128)(2,1)}), bf16[8192,256]{0,1:T(8,128)(2,1)}) %all-gather.6.cloned.1.call-update) | async-done | bytes 4194320 | tf_op jit(solution)/shard_map/all_gather | solution.py:268
  435.7 158.5 %while.44 = (s32[]{:T(128)}, f32[512]{0:T(512)S(1)}, f32[512]{0:T(512)S(1)}, f32[512,128]{1,0:T(8,128)S(1)}, f32[512]{0:T(512)S(1)}, /*index=5*/f32[512]{0:T(512...) while((s32[]{:T(128)}, f32[512]{0:T(512)S(1)}, ...), condition=%wide.region_15.17_spmd.clone, body=%wide.region_6.16_spmd.clone.sunk | while | flops 69732624 | bytes 3403379 | solution.py:275
  598.1 8.8 %collective-permute-done.3 = f32[512]{0:T(512)S(1)} collective-permute-done((f32[512]{0:T(512)S(1)}, f32[512]{0:T(512)S(1)}, u32[]{:S(2)}, u32[]{:S(2)}) %collective-permute-start.3) | collective-permute-done | bytes 2080 | tf_op jit(solution)/shard_map/ppermute | solution.py:28
  (959 shorter events, 309.6 us)
Async XLA Ops:
  6.5 346.5 %copy-start = (bf16[3584,128]{1,0:T(8,128)(2,1)S(1)}, bf16[3584,128]{1,0:T(8,128)(2,1)}, u32[]{:S(2)}) copy-start(bf16[3584,128]{1,0:T(8,128)(2,1)} %param.41) | copy-start | bytes 2752516
  6.5 98.1 %all-gather.10.cloned.1.call-start = ((), (), s32[]{:S(2)}) async-start(), calls=%async_computation.2 | async-start | bytes 16373760 | tf_op jit(solution)/shard_map/all_gather | solution.py:17
  9.1 329.0 %all-gather.8.cloned.1.call-start = ((), (), s32[]{:S(2)}) async-start(), calls=%async_computation.1 | async-start | bytes 1474560 | tf_op jit(solution)/shard_map/all_gather | solution.py:32
  138.6 1.4 copy-start.1
  138.6 1.4 copy-start.2
  138.6 1.4 copy-start.3
  149.4 15.1 %collective-permute-start = (bf16[243,1152]{1,0:T(8,128)(2,1)S(1)}, bf16[243,1152]{1,0:T(8,128)(2,1)S(1)}, u32[]{:S(2)}, u32[]{:S(2)}) collective-permute-start(bf16[243,1152]{1,0:T(8,128)(2,1)S(1)} %get-tuple-element.1143), channel_id=1, source_target_pairs={{0,64},{64,128},{128,192},{1,65},{65,129},{129,193},{2,66},{66,130... | collective-permute-start | bytes 1679624 | tf_op jit(solution)/shard_map/while/body/eval_jaxpr/ppermute | solution.py:28
  173.8 15.3 %collective-permute-start = (bf16[243,1152]{1,0:T(8,128)(2,1)S(1)}, bf16[243,1152]{1,0:T(8,128)(2,1)S(1)}, u32[]{:S(2)}, u32[]{:S(2)}) collective-permute-start(bf16[243,1152]{1,0:T(8,128)(2,1)S(1)} %get-tuple-element.1143), channel_id=1, source_target_pairs={{0,64},{64,128},{128,192},{1,65},{65,129},{129,193},{2,66},{66,130... | collective-permute-start | bytes 1679624 | tf_op jit(solution)/shard_map/while/body/eval_jaxpr/ppermute | solution.py:28
  198.4 14.4 %collective-permute-start = (bf16[243,1152]{1,0:T(8,128)(2,1)S(1)}, bf16[243,1152]{1,0:T(8,128)(2,1)S(1)}, u32[]{:S(2)}, u32[]{:S(2)}) collective-permute-start(bf16[243,1152]{1,0:T(8,128)(2,1)S(1)} %get-tuple-element.1143), channel_id=1, source_target_pairs={{0,64},{64,128},{128,192},{1,65},{65,129},{129,193},{2,66},{66,130... | collective-permute-start | bytes 1679624 | tf_op jit(solution)/shard_map/while/body/eval_jaxpr/ppermute | solution.py:28
  222.2 13.5 %collective-permute-start = (bf16[243,1152]{1,0:T(8,128)(2,1)S(1)}, bf16[243,1152]{1,0:T(8,128)(2,1)S(1)}, u32[]{:S(2)}, u32[]{:S(2)}) collective-permute-start(bf16[243,1152]{1,0:T(8,128)(2,1)S(1)} %get-tuple-element.1143), channel_id=1, source_target_pairs={{0,64},{64,128},{128,192},{1,65},{65,129},{129,193},{2,66},{66,130... | collective-permute-start | bytes 1679624 | tf_op jit(solution)/shard_map/while/body/eval_jaxpr/ppermute | solution.py:28
  245.1 12.7 %collective-permute-start = (bf16[243,1152]{1,0:T(8,128)(2,1)S(1)}, bf16[243,1152]{1,0:T(8,128)(2,1)S(1)}, u32[]{:S(2)}, u32[]{:S(2)}) collective-permute-start(bf16[243,1152]{1,0:T(8,128)(2,1)S(1)} %get-tuple-element.1143), channel_id=1, source_target_pairs={{0,64},{64,128},{128,192},{1,65},{65,129},{129,193},{2,66},{66,130... | collective-permute-start | bytes 1679624 | tf_op jit(solution)/shard_map/while/body/eval_jaxpr/ppermute | solution.py:28
  267.1 11.8 %collective-permute-start = (bf16[243,1152]{1,0:T(8,128)(2,1)S(1)}, bf16[243,1152]{1,0:T(8,128)(2,1)S(1)}, u32[]{:S(2)}, u32[]{:S(2)}) collective-permute-start(bf16[243,1152]{1,0:T(8,128)(2,1)S(1)} %get-tuple-element.1143), channel_id=1, source_target_pairs={{0,64},{64,128},{128,192},{1,65},{65,129},{129,193},{2,66},{66,130... | collective-permute-start | bytes 1679624 | tf_op jit(solution)/shard_map/while/body/eval_jaxpr/ppermute | solution.py:28
  295.1 8.4 %collective-permute-start.1 = (bf16[128,1152]{1,0:T(8,128)(2,1)S(1)}, bf16[128,1152]{1,0:T(8,128)(2,1)S(1)}, u32[]{:S(2)}, u32[]{:S(2)}) collective-permute-start(bf16[128,1152]{1,0:T(8,128)(2,1)S(1)} %select_select_fusion), channel_id=1, source_target_pairs={{0,1},{1,2},{2,3},{3,4},{4,5},{5,6},{6,7},{7,8},{8,9},{9,10},{10,1... | collective-permute-start | bytes 884744 | tf_op jit(solution)/shard_map/ppermute | solution.py:28
  304.4 131.2 %all-gather.6.cloned.1.call-start = ((), (), s32[]{:S(2)}) async-start(), calls=%async_computation | async-start | bytes 4259840 | tf_op jit(solution)/shard_map/all_gather | solution.py:268
  338.1 15.0 %copy-start.5 = (f32[3584]{0:T(1024)S(1)}, f32[3584]{0:T(1024)}, u32[]{:S(2)}) copy-start(f32[3584]{0:T(1024)} %param.38) | copy-start | bytes 43012
  340.2 13.4 %copy-start.4 = (bf16[3584,128]{1,0:T(8,128)(2,1)S(1)}, bf16[3584,128]{1,0:T(8,128)(2,1)}, u32[]{:S(2)}) copy-start(bf16[3584,128]{1,0:T(8,128)(2,1)} %param.42) | copy-start | bytes 2752516
  340.3 13.4 %copy-start.7 = (f32[128]{0:T(128)S(1)}, f32[128]{0:T(128)}, u32[]{:S(2)}) copy-start(f32[128]{0:T(128)} %param.43) | copy-start | bytes 1540
  353.1 2.4 copy-start.6
  358.7 6.5 %collective-permute-start.2 = (bf16[512,128]{1,0:T(8,128)(2,1)S(1)}, bf16[512,128]{1,0:T(8,128)(2,1)S(1)}, u32[]{:S(2)}, u32[]{:S(2)}) collective-permute-start(bf16[512,128]{1,0:T(8,128)(2,1)S(1)} %pad_maximum_fusion), channel_id=1, source_target_pairs={{32,0},{33,1},{34,2},{35,3},{36,4},{37,5},{38,6},{39,7},{40,8},{41... | collective-permute-start | bytes 393224 | tf_op jit(solution)/shard_map/ppermute | solution.py:28
  594.2 12.8 %collective-permute-start.4 = (f32[512,128]{1,0:T(8,128)S(1)}, f32[512,128]{1,0:T(8,128)S(1)}, u32[]{:S(2)}, u32[]{:S(2)}) collective-permute-start(f32[512,128]{1,0:T(8,128)S(1)} %get-tuple-element.732), channel_id=1, source_target_pairs={{0,32},{1,33},{2,34},{3,35},{4,36},{5,37},{6,38},{7,39},{8,40},{9,... | collective-permute-start | bytes 786440 | tf_op jit(solution)/shard_map/ppermute | solution.py:28
  595.5 11.4 %collective-permute-start.3 = (f32[512]{0:T(512)S(1)}, f32[512]{0:T(512)S(1)}, u32[]{:S(2)}, u32[]{:S(2)}) collective-permute-start(f32[512]{0:T(512)S(1)} %get-tuple-element.731), channel_id=1, source_target_pairs={{0,32},{1,33},{2,34},{3,35},{4,36},{5,37},{6,38},{7,39},{8,40},{9,... | collective-permute-start | bytes 6152 | tf_op jit(solution)/shard_map/ppermute | solution.py:28
  596.8 10.1 %collective-permute-start.5 = (f32[512]{0:T(512)S(1)}, f32[512]{0:T(512)S(1)}, u32[]{:S(2)}, u32[]{:S(2)}) collective-permute-start(f32[512]{0:T(512)S(1)} %get-tuple-element.734), channel_id=1, source_target_pairs={{0,32},{1,33},{2,34},{3,35},{4,36},{5,37},{6,38},{7,39},{8,40},{9,... | collective-permute-start | bytes 6152 | tf_op jit(solution)/shard_map/ppermute | solution.py:28
Sparse Core Ops, SparseCore 0:
  10.1 94.4 all-gather.9
  304.5 33.4 all-gather.7
  355.3 80.2 all-gather.5
where the time goes:
time: 621 us; the launch traced here: 615 us
  waiting for transfers between devices  246 us (40%)
  local copies, waits for them, and re-layouts  188 us (30%)
  matrix products  78.1 us (13%)
  other arithmetic  34.1 us (5%)
  starting transfers between devices  33.8 us (5%)
  between operations  13.5 us (2%)
  blocking collectives  12.5 us (2%)
  loops' own time  8.41 us (1%)
    all_gather x1, waiting for transfers between devices, turned_gather(): lax.all_gather(both, axis, axis=0, tiled=True)  91.2 us
    all_gather x1, waiting for transfers between devices, per_device(): arrived_rows = lax.all_gather(stacked, 'seq', axis=0, tiled=True)  70.4 us
    dynamic_slice x128, local copies, waits for them, and re-layouts, visit_one(): lax.dynamic_slice_in_dim(arrived_rows, block_index * sub_rows, sub_rows, 0)  61.2 us
    ppermute x11, waiting for transfers between devices, passed_along(): return lax.ppermute(block, axis, route)  51.2 us
    dot_general x6, matrix products, encoder_layer(): jnp.dot(hidden, w_out, preferred_element_type=jnp.float32)  45.1 us
    dynamic_slice x48, local copies, waits for them, and re-layouts, attend_block(): lax.dynamic_slice_in_dim(segment_ids, block_start, key_block.shape[0], 0)  36.7 us
    ppermute x11, starting transfers between devices, passed_along(): return lax.ppermute(block, axis, route)  33.6 us
    all_gather x1, waiting for transfers between devices, from_root(): lax.all_gather(x, axis)  33.4 us
  transfers between devices with their start and end apart: 14, of which 12 were waited for; matrix products, arithmetic and copies ran while one was open for 5% of the time, Pallas kernels for 0%

commit v1 on v0

--- a/solution.py
+++ b/solution.py
@@ -14,7 +14,13 @@
 def turned_gather(arrays, axis, dims):
     turned = [jnp.moveaxis(a, dim, 0) for a, dim in zip(arrays, dims)]
     both = jnp.concatenate([t.reshape(len(t), -1) for t in turned], axis=1)
-    filled, at, finished = (lax.all_gather(both, axis, axis=0, tiled=True), 0, [])
+    filled, at, finished = (
+        jnp.concatenate(
+            lax.all_to_all(jnp.stack([both] * lax.axis_size(axis)), axis, 0, 0), axis=0
+        ),
+        0,
+        [],
+    )
     for t, dim in zip(turned, dims):
         section = filled[:, at : at + t[0].size].reshape(-1, *t.shape[1:])
         finished.append(jnp.moveaxis(section, 0, dim))

time: 621 us -> 891 us (1.43)
  waiting for transfers between devices: 246 us -> 503 us
  starting transfers between devices: 33.8 us -> 43.4 us
    all_to_all x0 -> x1, waiting for transfers between devices: none -> 343 us  [turned_gather(): lax.all_to_all(jnp.stack([both] * lax.axis_size(axis)), axis, 0, 0)]
    all_gather x1 -> x0, waiting for transfers between devices: 91.2 us -> none  [turned_gather(): lax.all_gather(both, axis, axis=0, tiled=True)]
    reshape x0 -> x1, local copies, waits for them, and re-layouts: none -> 17.1 us  [turned_gather(): jnp.concatenate(lax.all_to_all(jnp.stack([both] * lax.axis_size(axis)), a...]
    unnamed x17 -> x20, local copies, waits for them, and re-layouts: 17.1 us -> 0.05 us
    all_to_all x0 -> x1, starting transfers between devices: none -> 9.66 us  [turned_gather(): lax.all_to_all(jnp.stack([both] * lax.axis_size(axis)), axis, 0, 0)]
  transfers between devices with their start and end apart: 14 -> 14, of which waited for: 12 -> 12; matrix products, arithmetic and copies ran while one was open for 5% -> 4% of each run, Pallas kernels for 0% -> 0%
where the time goes in v1:
time: 891 us; the launch traced here: 885 us
  waiting for transfers between devices  503 us (56%)
  local copies, waits for them, and re-layouts  192 us (22%)
  matrix products  78.2 us (9%)
  starting transfers between devices  43.4 us (5%)
  other arithmetic  33.5 us (4%)
  between operations  13.8 us (2%)
  blocking collectives  12.7 us (1%)
    all_to_all x1, waiting for transfers between devices, turned_gather(): lax.all_to_all(jnp.stack([both] * lax.axis_size(axis)), axis, 0, 0)  343 us
    all_gather x1, waiting for transfers between devices, per_device(): arrived_rows = lax.all_gather(stacked, 'seq', axis=0, tiled=True)  70.4 us
    dynamic_slice x128, local copies, waits for them, and re-layouts, visit_one(): lax.dynamic_slice_in_dim(arrived_rows, block_index * sub_rows, sub_rows, 0)  61.2 us
    ppermute x11, waiting for transfers between devices, passed_along(): return lax.ppermute(block, axis, route)  47.4 us
    dot_general x6, matrix products, encoder_layer(): jnp.dot(hidden, w_out, preferred_element_type=jnp.float32)  45.1 us
    all_gather x1, waiting for transfers between devices, from_root(): lax.all_gather(x, axis)  41.9 us
    dynamic_slice x48, local copies, waits for them, and re-layouts, attend_block(): lax.dynamic_slice_in_dim(segment_ids, block_start, key_block.shape[0], 0)  36.7 us
    ppermute x11, starting transfers between devices, passed_along(): return lax.ppermute(block, axis, route)  33.6 us
  transfers between devices with their start and end apart: 14, of which 12 were waited for; matrix products, arithmetic and copies ran while one was open for 4% of the time, Pallas kernels for 0%

profile of v1, /device:TPU:231, one launch (start us, length us, event | category | flops | bytes accessed | tf_op | source)
XLA Modules:
  0.0 884.7 jit_solution(16243551358765664413)
XLA Ops:
  8.4 5.8 stack.2
  14.2 9.7 %all-to-all-start = ((bf16[64,18,5248]{2,1,0:T(8,128)(2,1)}), bf16[64,18,5248]{2,1,0:T(8,128)(2,1)}, u32[]{:S(2)}, u32[]{:S(2)}) async-start(bf16[64,18,5248]{2,1,0:T(8,128)(2,1)} %stack.2), calls=%async_computation | async-start | bytes 32243712 | tf_op jit(solution)/shard_map/all_to_all | solution.py:19
  26.8 342.9 %all-to-all-done = bf16[64,18,5248]{2,1,0:T(8,128)(2,1)} async-done(((bf16[64,18,5248]{2,1,0:T(8,128)(2,1)}), bf16[64,18,5248]{2,1,0:T(8,128)(2,1)}, u32[]{:S(2)}, u32[]{:S(2)}) %all-to-all-start) | async-done | bytes 12091424 | tf_op jit(solution)/shard_map/all_to_all | solution.py:19
  369.7 17.1 %reshape.270 = bf16[1152,5248]{1,0:T(8,128)(2,1)} reshape(bf16[64,18,5248]{2,1,0:T(8,128)(2,1)} %all-to-all-done) | data formatting | bytes 24182784 | tf_op jit(solution)/shard_map/reshape | solution.py:18
  386.8 8.4 slice_bitcast_fusion
  395.2 8.4 copy.21
  405.0 134.5 %while.43 = (s32[]{:T(128)}, bf16[243,1152]{1,0:T(8,128)(2,1)S(1)}, bf16[729,1152]{1,0:T(8,128)(2,1)}, pred[]{:T(512)}, bf16[729,1152]{1,0:T(8,128)(2,1)}, /*ind...) while((s32[]{:T(128)}, bf16[243,1152]{1,0:T(8,128)(2,1)S(1)}, ...), condition=%wide.region_3.4_spmd, body=%wide.region_0.3_spmd.sunk | while | flops 2446610432 | bytes 18521884 | solution.py:185
  406.9 7.5 dynamic-slice_select_fusion.4
  421.1 7.8 collective-permute-done
  430.7 7.5 dynamic-slice_select_fusion.4
  438.2 4.1 collective-permute-start
  445.8 6.9 collective-permute-done
  454.5 7.5 dynamic-slice_select_fusion.4
  462.0 4.1 collective-permute-start
  469.6 6.1 collective-permute-done
  477.5 7.5 dynamic-slice_select_fusion.4
  485.0 4.1 collective-permute-start
  492.6 5.2 collective-permute-done
  499.6 7.5 dynamic-slice_select_fusion.4
  507.2 4.1 collective-permute-start
  514.8 4.4 collective-permute-done
  520.9 7.5 dynamic-slice_select_fusion.4
  528.4 4.1 collective-permute-start
  544.4 5.5 reshape.279
  549.9 4.5 reduce_sum.76
  561.2 3.7 collective-permute-done.1
  565.9 41.9 %all-gather.6.cloned.1.call-done = bf16[512,1152]{1,0:T(8,128)(2,1)} async-done(((bf16[128,1152]{1,0:T(8,128)(2,1)}), bf16[512,1152]{1,0:T(8,128)(2,1)}) %all-gather.6.cloned.1.call-update) | async-done | bytes 1179664 | tf_op jit(solution)/shard_map/all_gather | solution.py:38
  609.9 12.7 %all_gather.14 = bf16[128,3584]{1,0:T(8,128)(2,1)S(1)} all-gather(bf16[128,896]{1,0:T(8,128)(2,1)S(1)} %fusion.69), channel_id=1, replica_groups=mesh['section'=4,'seq'=64] {'section'}, dimensions={1}, use_global_device_ids=true | all-gather | bytes 1146880 | tf_op jit(solution)/shard_map/all_gather | solution.py:202
  628.6 4.5 collective-permute-start.2
  635.0 70.4 %all-gather.4.cloned.1.call-done = bf16[8192,256]{0,1:T(8,128)(2,1)} async-done(((bf16[128,256]{0,1:T(8,128)(2,1)}), bf16[8192,256]{0,1:T(8,128)(2,1)}) %all-gather.4.cloned.1.call-update) | async-done | bytes 4194320 | tf_op jit(solution)/shard_map/all_gather | solution.py:274
  705.5 158.5 %while.44 = (s32[]{:T(128)}, f32[512]{0:T(512)S(1)}, f32[512]{0:T(512)S(1)}, f32[512,128]{1,0:T(8,128)S(1)}, f32[512]{0:T(512)S(1)}, /*index=5*/f32[512]{0:T(512...) while((s32[]{:T(128)}, f32[512]{0:T(512)S(1)}, ...), condition=%wide.region_15.17_spmd.clone, body=%wide.region_6.16_spmd.clone.sunk | while | flops 69732624 | bytes 3403379 | solution.py:281
  868.0 8.8 collective-permute-done.3
  (963 shorter events, 314.8 us)
Async XLA Ops:
  6.5 616.4 %copy-start = (bf16[3584,128]{1,0:T(8,128)(2,1)S(1)}, bf16[3584,128]{1,0:T(8,128)(2,1)}, u32[]{:S(2)}) copy-start(bf16[3584,128]{1,0:T(8,128)(2,1)} %param.41) | copy-start | bytes 2752516
  14.2 10.0 %copy-start.4 = (s32[64]{0:T(128)S(1)}, s32[64]{0:T(128)}, u32[]{:S(2)}) copy-start(s32[64]{0:T(128)} %param.35) | copy-start | bytes 772
  14.2 10.7 %copy-start.5 = (s32[64]{0:T(128)S(1)}, s32[64]{0:T(128)}, u32[]{:S(2)}) copy-start(s32[64]{0:T(128)} %param.36) | copy-start | bytes 772
  14.2 355.5 %all-to-all-start = ((bf16[64,18,5248]{2,1,0:T(8,128)(2,1)}), bf16[64,18,5248]{2,1,0:T(8,128)(2,1)}, u32[]{:S(2)}, u32[]{:S(2)}) async-start(bf16[64,18,5248]{2,1,0:T(8,128)(2,1)} %stack.2), calls=%async_computation | async-start | bytes 32243712 | tf_op jit(solution)/shard_map/all_to_all | solution.py:19
  23.9 583.8 %all-gather.6.cloned.1.call-start = ((), (), s32[]{:S(2)}) async-start(), calls=%async_computation.2 | async-start | bytes 1474560 | tf_op jit(solution)/shard_map/all_gather | solution.py:38
  403.6 1.4 copy-start.1
  403.6 1.4 copy-start.2
  403.6 1.4 copy-start.3
  414.4 14.5 %collective-permute-start = (bf16[243,1152]{1,0:T(8,128)(2,1)S(1)}, bf16[243,1152]{1,0:T(8,128)(2,1)S(1)}, u32[]{:S(2)}, u32[]{:S(2)}) collective-permute-start(bf16[243,1152]{1,0:T(8,128)(2,1)S(1)} %get-tuple-element.1114), channel_id=1, source_target_pairs={{0,64},{64,128},{128,192},{1,65},{65,129},{129,193},{2,66},{66,130... | collective-permute-start | bytes 1679624 | tf_op jit(solution)/shard_map/while/body/eval_jaxpr/ppermute | solution.py:34
  438.2 14.5 %collective-permute-start = (bf16[243,1152]{1,0:T(8,128)(2,1)S(1)}, bf16[243,1152]{1,0:T(8,128)(2,1)S(1)}, u32[]{:S(2)}, u32[]{:S(2)}) collective-permute-start(bf16[243,1152]{1,0:T(8,128)(2,1)S(1)} %get-tuple-element.1114), channel_id=1, source_target_pairs={{0,64},{64,128},{128,192},{1,65},{65,129},{129,193},{2,66},{66,130... | collective-permute-start | bytes 1679624 | tf_op jit(solution)/shard_map/while/body/eval_jaxpr/ppermute | solution.py:34
  462.0 13.7 %collective-permute-start = (bf16[243,1152]{1,0:T(8,128)(2,1)S(1)}, bf16[243,1152]{1,0:T(8,128)(2,1)S(1)}, u32[]{:S(2)}, u32[]{:S(2)}) collective-permute-start(bf16[243,1152]{1,0:T(8,128)(2,1)S(1)} %get-tuple-element.1114), channel_id=1, source_target_pairs={{0,64},{64,128},{128,192},{1,65},{65,129},{129,193},{2,66},{66,130... | collective-permute-start | bytes 1679624 | tf_op jit(solution)/shard_map/while/body/eval_jaxpr/ppermute | solution.py:34
  485.0 12.8 %collective-permute-start = (bf16[243,1152]{1,0:T(8,128)(2,1)S(1)}, bf16[243,1152]{1,0:T(8,128)(2,1)S(1)}, u32[]{:S(2)}, u32[]{:S(2)}) collective-permute-start(bf16[243,1152]{1,0:T(8,128)(2,1)S(1)} %get-tuple-element.1114), channel_id=1, source_target_pairs={{0,64},{64,128},{128,192},{1,65},{65,129},{129,193},{2,66},{66,130... | collective-permute-start | bytes 1679624 | tf_op jit(solution)/shard_map/while/body/eval_jaxpr/ppermute | solution.py:34
  507.2 11.9 %collective-permute-start = (bf16[243,1152]{1,0:T(8,128)(2,1)S(1)}, bf16[243,1152]{1,0:T(8,128)(2,1)S(1)}, u32[]{:S(2)}, u32[]{:S(2)}) collective-permute-start(bf16[243,1152]{1,0:T(8,128)(2,1)S(1)} %get-tuple-element.1114), channel_id=1, source_target_pairs={{0,64},{64,128},{128,192},{1,65},{65,129},{129,193},{2,66},{66,130... | collective-permute-start | bytes 1679624 | tf_op jit(solution)/shard_map/while/body/eval_jaxpr/ppermute | solution.py:34
  528.4 11.1 %collective-permute-start = (bf16[243,1152]{1,0:T(8,128)(2,1)S(1)}, bf16[243,1152]{1,0:T(8,128)(2,1)S(1)}, u32[]{:S(2)}, u32[]{:S(2)}) collective-permute-start(bf16[243,1152]{1,0:T(8,128)(2,1)S(1)} %get-tuple-element.1114), channel_id=1, source_target_pairs={{0,64},{64,128},{128,192},{1,65},{65,129},{129,193},{2,66},{66,130... | collective-permute-start | bytes 1679624 | tf_op jit(solution)/shard_map/while/body/eval_jaxpr/ppermute | solution.py:34
  555.7 9.1 %collective-permute-start.1 = (bf16[128,1152]{1,0:T(8,128)(2,1)S(1)}, bf16[128,1152]{1,0:T(8,128)(2,1)S(1)}, u32[]{:S(2)}, u32[]{:S(2)}) collective-permute-start(bf16[128,1152]{1,0:T(8,128)(2,1)S(1)} %select_select_fusion), channel_id=1, source_target_pairs={{0,1},{1,2},{2,3},{3,4},{4,5},{5,6},{6,7},{7,8},{8,9},{9,10},{10,1... | collective-permute-start | bytes 884744 | tf_op jit(solution)/shard_map/ppermute | solution.py:34
  565.8 139.6 %all-gather.4.cloned.1.call-start = ((), (), s32[]{:S(2)}) async-start(), calls=%async_computation.1 | async-start | bytes 4259840 | tf_op jit(solution)/shard_map/all_gather | solution.py:274
  607.7 15.2 %copy-start.7 = (f32[3584]{0:T(1024)S(1)}, f32[3584]{0:T(1024)}, u32[]{:S(2)}) copy-start(f32[3584]{0:T(1024)} %param.38) | copy-start | bytes 43012
  609.9 13.6 %copy-start.6 = (bf16[3584,128]{1,0:T(8,128)(2,1)S(1)}, bf16[3584,128]{1,0:T(8,128)(2,1)}, u32[]{:S(2)}) copy-start(bf16[3584,128]{1,0:T(8,128)(2,1)} %param.42) | copy-start | bytes 2752516
  609.9 13.6 %copy-start.9 = (f32[128]{0:T(128)S(1)}, f32[128]{0:T(128)}, u32[]{:S(2)}) copy-start(f32[128]{0:T(128)} %param.43) | copy-start | bytes 1540
  622.9 2.4 copy-start.8
  628.6 6.5 collective-permute-start.2
  864.1 12.8 %collective-permute-start.4 = (f32[512,128]{1,0:T(8,128)S(1)}, f32[512,128]{1,0:T(8,128)S(1)}, u32[]{:S(2)}, u32[]{:S(2)}) collective-permute-start(f32[512,128]{1,0:T(8,128)S(1)} %get-tuple-element.732), channel_id=1, source_target_pairs={{0,32},{1,33},{2,34},{3,35},{4,36},{5,37},{6,38},{7,39},{8,40},{9,... | collective-permute-start | bytes 786440 | tf_op jit(solution)/shard_map/ppermute | solution.py:34
  865.4 11.4 %collective-permute-start.3 = (f32[512]{0:T(512)S(1)}, f32[512]{0:T(512)S(1)}, u32[]{:S(2)}, u32[]{:S(2)}) collective-permute-start(f32[512]{0:T(512)S(1)} %get-tuple-element.731), channel_id=1, source_target_pairs={{0,32},{1,33},{2,34},{3,35},{4,36},{5,37},{6,38},{7,39},{8,40},{9,... | collective-permute-start | bytes 6152 | tf_op jit(solution)/shard_map/ppermute | solution.py:34
  866.7 10.1 %collective-permute-start.5 = (f32[512]{0:T(512)S(1)}, f32[512]{0:T(512)S(1)}, u32[]{:S(2)}, u32[]{:S(2)}) collective-permute-start(f32[512]{0:T(512)S(1)} %get-tuple-element.734), channel_id=1, source_target_pairs={{0,32},{1,33},{2,34},{3,35},{4,36},{5,37},{6,38},{7,39},{8,40},{9,... | collective-permute-start | bytes 6152 | tf_op jit(solution)/shard_map/ppermute | solution.py:34
Sparse Core Ops, SparseCore 0:
  565.9 41.7 all-gather.5
  625.1 80.2 all-gather.3
